TPU v7x, 32 devices: a whole 2x2x4 slice. The times are simulated.
32 devices in a mesh: grp: 2 (over y), gx: 4 (over z), gy: 2 (over x), gz: 2 (over core).
Axes of the slice: x: 2, y: 2, z: 4, core: 2. Of those that a mesh axis runs over, the one named last changes fastest.
Arguments:
- observed: float32 [2048, 4, 256], P(('grp', 'gx', 'gy', 'gz')), parts along dimension 0, may hold values from -12 to 12
- predicted: float32 [2048, 4, 256], P(('grp', 'gx', 'gy', 'gz')), parts along dimension 0, may hold values from -6 to 6
- coherence_mask: int32 [2048, 256], P(('grp', 'gx', 'gy', 'gz')), parts along dimension 0, may hold values 0 or 1
- block_count: int32 [2048], P(('grp', 'gx', 'gy', 'gz')), parts along dimension 0, may hold values from 64 to 256
- block_owner: int32 [2048, 1], P(('grp', 'gx', 'gy', 'gz')), parts along dimension 0, may hold values from 0 to 7; in each aligned block of 64 rows (0 to 63, 64 to 127, ...) at most 16 rows name the same one
- block_matrix_choice: int32 [2048], P(('grp', 'gx', 'gy', 'gz')), parts along dimension 0, may hold values from 0 to 31
- block_patch: int32 [2048], P(('grp', 'gx', 'gy', 'gz')), parts along dimension 0, may hold values from 0 to 31
- look_vector: float32 [4, 3], replicated, may hold values from -1 to 1
- interp_weights: bfloat16 [32, 256, 128], replicated, may hold values from -0.375 to 0.375
- depth_kernel: float32 [64], P(('grp', 'gz')), parts along dimension 0, may hold values from 0.2 to 1
- stiffness: float32 [64, 128, 256], P(('grp', 'gz'), 'gx', 'gy'), parts along dimension 0, may hold values from 0.25 to 4
Outputs:
- adjoint_field: float32 [3, 64, 128, 256], P(None, ('grp', 'gz'), 'gx', 'gy'), parts along dimension 1
- cg_residual: float32 [3, 64, 128, 256], P(None, ('grp', 'gz'), 'gx', 'gy'), parts along dimension 1
There are 2 independent parts, one for each index of `grp`. A program takes and returns all parts, laid end to end along the dimension named above; an argument that names none is the same for every part. Nothing has to cross between parts.
Inputs may be any that keep to these rules, and one draw needn't show every extreme that they name: `block_owner`: the blocks of one device name no column tile more than 16 times; in some devices one tile is named exactly 16 times.
All inputs are finite; a program needn't handle non-finite values. No bound on the sum of `coherence_mask` on one device may be relied on, other than what follows from the above.
Results may differ from a plain program's by a relative error of at most 0.0029.
Values sent between devices are 32-bit elements; how exact they have to be, the bound alone decides.
A program may use at most 64 MiB of HBM per device.

v0:
```python
import math
import jax
import jax.numpy as jnp
from jax import lax
from jax.sharding import PartitionSpec as P

EPOCHS = 4
PATCH_X = 8
PATCH_Y = 16
ITERS = 3
KAPPA = 0.5
EPS = 1e-06
SPATIAL = (1, 2, 0)


def extended(cells, sides, width):
    for axis, dim in sides:
        count = lax.axis_size(axis)
        ends = count - 1
        head = lax.slice_in_dim(cells, 0, width, axis=dim)
        tail = lax.slice_in_dim(cells, cells.shape[dim] - width, cells.shape[dim], axis=dim)
        cells = jnp.concatenate(
            [
                lax.ppermute(tail, axis, [(i, (i + 1) % count) for i in range(ends)]),
                cells,
                lax.ppermute(head, axis, [((i + 1) % count, i) for i in range(ends)]),
            ],
            axis=dim,
        )
    return cells


def beside_all(padded):
    total = padded[2:, 1:-1, 1:-1] + padded[:-2, 1:-1, 1:-1]
    total = total + padded[1:-1, 2:, 1:-1] + padded[1:-1, :-2, 1:-1]
    return total + padded[1:-1, 1:-1, 2:] + padded[1:-1, 1:-1, :-2]


def central(padded, axis):
    if axis == 0:
        return 0.5 * (padded[2:, 1:-1, 1:-1] - padded[:-2, 1:-1, 1:-1])
    if axis == 1:
        return 0.5 * (padded[1:-1, 2:, 1:-1] - padded[1:-1, :-2, 1:-1])
    return 0.5 * (padded[1:-1, 1:-1, 2:] - padded[1:-1, 1:-1, :-2])


def operate(field, stiffness):
    padded = extended(field, (("gx", 2), ("gy", 3), ("gz", 1)), 1)
    spread = (
        central(padded[0], SPATIAL[0])
        + central(padded[1], SPATIAL[1])
        + central(padded[2], SPATIAL[2])
    )
    spread_pad = extended(spread, (("gx", 1), ("gy", 2), ("gz", 0)), 1)
    parts = [
        (6.0 + stiffness) * field[member]
        - beside_all(padded[member])
        - KAPPA * central(spread_pad, SPATIAL[member])
        for member in range(3)
    ]
    return jnp.stack(parts)


def project(resid, look_vector):
    return jnp.einsum("ec,nep->ncp", look_vector, resid, precision=lax.Precision.HIGHEST).astype(
        jnp.bfloat16
    )


def contribute(coeffs, tables, weights):
    total = coeffs.shape[0]
    group = math.gcd(total, 32)
    coefficient_sets = coeffs.reshape(total // group, group, 3, coeffs.shape[2])
    table_groups = tables.reshape(total // group, group)

    def per_group(both_parts):
        block_coefficient_values, block_tables = both_parts
        selected_entries = jnp.take(weights, block_tables, axis=0)
        return jnp.einsum(
            "aow,awv->aov",
            block_coefficient_values,
            selected_entries,
            preferred_element_type=jnp.float32,
        )

    result = lax.map(per_group, (coefficient_sets, table_groups))
    return result.reshape(total, 3, weights.shape[2])


def two_products(residual, image):
    return lax.psum((jnp.sum(residual * residual), jnp.sum(residual * image)), ("gx", "gy", "gz"))


def per_device(
    observed,
    predicted,
    coherence_mask,
    block_count,
    block_owner,
    block_matrix_choice,
    block_patch,
    look_vector,
    interp_weights,
    depth_kernel,
    stiffness,
):
    blocks = observed.shape[0]
    pixels = observed.shape[2]
    cells = PATCH_X * PATCH_Y
    owners = lax.axis_size("gx") * lax.axis_size("gy")
    capacity = max(4, 2 * blocks // owners)
    slots = owners * capacity
    local_x = stiffness.shape[1]
    local_y = stiffness.shape[2]
    places_x = local_x // PATCH_X
    northing_places = local_y // PATCH_Y
    places = places_x * northing_places
    column = lax.broadcasted_iota(jnp.int32, (blocks, pixels), 1)
    valid = coherence_mask.astype(jnp.float32) * (column < block_count[:, None]).astype(jnp.float32)
    resid = (predicted - observed) * valid[:, None, :]
    misfit, weight = lax.psum((jnp.sum(resid * resid), jnp.sum(valid)), ("gx", "gy", "gz"))
    scale = lax.rsqrt(misfit / (EPOCHS * weight) + EPS)
    owner = block_owner[:, 0]
    order = lax.broadcasted_iota(jnp.int32, (blocks, blocks), 0)
    other = lax.broadcasted_iota(jnp.int32, (blocks, blocks), 1)
    earlier = (owner[:, None] == owner[None, :]) & (other < order)
    rank = jnp.sum(earlier.astype(jnp.int32), axis=1)
    slot = owner * capacity + rank
    slot_ids = lax.broadcasted_iota(jnp.int32, (blocks, slots), 1)
    chosen = slot_ids == slot[:, None]
    select = chosen.astype(jnp.float32)
    patch_slot = jnp.sum(jnp.where(chosen, block_patch[:, None], 0), axis=0).reshape(
        owners, capacity
    )
    table_slot = jnp.sum(jnp.where(chosen, block_matrix_choice[:, None], 0), axis=0).reshape(
        owners, capacity
    )
    resid_slot = jnp.einsum("bs,bep->sep", select, resid, precision=lax.Precision.HIGHEST).reshape(
        owners, capacity, EPOCHS, pixels
    )
    arrived = lax.all_to_all(resid_slot, ("gx", "gy"), split_axis=0, concat_axis=0, tiled=True)
    tables = lax.all_to_all(table_slot, ("gx", "gy"), split_axis=0, concat_axis=0, tiled=True)
    patches = lax.all_to_all(patch_slot, ("gx", "gy"), split_axis=0, concat_axis=0, tiled=True)
    sources = tables.shape[0]
    width = tables.shape[1]
    coeffs = project(arrived.reshape(sources * width, EPOCHS, pixels), look_vector)
    sums = contribute(coeffs, tables.reshape(sources * width), interp_weights)
    patch_total_sums = sums.reshape(sources, width, 3, cells)
    flat_sums = patch_total_sums.reshape(slots, 3, cells)
    flat_ids = patches.reshape(slots)
    place_ids = lax.broadcasted_iota(jnp.int32, (slots, places), 1)
    onehot = (flat_ids[:, None] == place_ids).astype(jnp.float32)
    placed = jnp.einsum("np,ncs->pcs", onehot, flat_sums, precision=lax.Precision.HIGHEST)
    surface = (
        placed.reshape(places_x, northing_places, 3, PATCH_X, PATCH_Y)
        .transpose(2, 0, 3, 1, 4)
        .reshape(3, local_x, local_y)
    )
    surface = lax.psum(surface, "gz")
    source = scale * depth_kernel[None, :, None, None] * surface[:, None, :, :]
    adjoint_field = jnp.zeros_like(source)
    cg_residual = source
    image = operate(cg_residual, stiffness)
    norm_now, product = two_products(cg_residual, image)
    alpha = norm_now / product
    direction = cg_residual
    along = image
    for step in range(ITERS):
        adjoint_field = adjoint_field + alpha * direction
        cg_residual = cg_residual - alpha * along
        if step + 1 < ITERS:
            image = operate(cg_residual, stiffness)
            norm_next, product = two_products(cg_residual, image)
            ratio = norm_next / norm_now
            alpha = norm_next / (product - ratio * norm_next / alpha)
            direction = cg_residual + ratio * direction
            along = image + ratio * along
            norm_now = norm_next
    return (adjoint_field, cg_residual)


def solution(mesh):
    in_specs = (
        P(("grp", "gx", "gy", "gz"), None, None),
        P(("grp", "gx", "gy", "gz"), None, None),
        P(("grp", "gx", "gy", "gz"), None),
        P(("grp", "gx", "gy", "gz")),
        P(("grp", "gx", "gy", "gz"), None),
        P(("grp", "gx", "gy", "gz")),
        P(("grp", "gx", "gy", "gz")),
        P(),
        P(),
        P(("grp", "gz")),
        P(("grp", "gz"), "gx", "gy"),
    )
    out_specs = (P(None, ("grp", "gz"), "gx", "gy"), P(None, ("grp", "gz"), "gx", "gy"))
    return jax.shard_map(
        per_device, mesh=mesh, in_specs=in_specs, out_specs=out_specs, check_vma=False
    )
```

profile of v0, /device:TPU:0, one launch (start us, length us, event | category | flops | bytes accessed | tf_op | source)
XLA Modules:
  0.0 349.5 jit_solution(3229247939557360916)
XLA Ops:
  3.7 7.3 %all-to-all-start.2 = ((s32[8,1,16]{2,1,0:T(1,128)}), s32[8,1,16]{2,1,0:T(1,128)S(1)}, u32[]{:S(2)}, u32[]{:S(2)}) async-start(s32[8,1,16]{2,1,0:T(1,128)} %bitcast.17), calls=%async_computation.2 | async-start | bytes 8192 | tf_op jit(solution)/shard_map/all_to_all | solution.py:142
  17.4 3.6 %all-to-all-start = ((s32[8,1,16]{2,1,0:T(1,128)}), s32[8,1,16]{2,1,0:T(1,128)S(1)}, u32[]{:S(2)}, u32[]{:S(2)}) async-start(s32[8,1,16]{2,1,0:T(1,128)} %bitcast.8), calls=%async_computation | async-start | bytes 8192 | tf_op jit(solution)/shard_map/all_to_all | solution.py:143
  22.4 5.1 %all-to-all-done = s32[8,1,16]{2,1,0:T(1,128)S(1)} async-done(((s32[8,1,16]{2,1,0:T(1,128)}), s32[8,1,16]{2,1,0:T(1,128)S(1)}, u32[]{:S(2)}, u32[]{:S(2)}) %all-to-all-start) | async-done | bytes 544 | tf_op jit(solution)/shard_map/all_to_all | solution.py:143
  27.4 3.5 %all-to-all-start.1 = ((f32[8,16,4,256]{3,1,2,0:T(8,128)}), f32[8,16,4,256]{3,1,2,0:T(8,128)S(1)}, u32[]{:S(2)}, u32[]{:S(2)}) async-start(f32[8,16,4,256]{3,1,2,0:T(8,128)} %copy.111), calls=%async_computation.1 | async-start | bytes 1048576 | tf_op jit(solution)/shard_map/all_to_all | solution.py:141
  31.0 34.7 %all-reduce.3 = (f32[]{:T(128)}, f32[]{:T(128)}) all-reduce(f32[]{:T(128)} %get-tuple-element.64, f32[]{:T(128)} %get-tuple-element.62), channel_id=1, replica_groups=mesh['grp'=2,'gx'=4,'gy'=2,'gz'=2] {'gx','gy','gz'}, use_global_device_ids=true, to_apply=%region_1.0 | all-reduce | flops 2 | bytes 16 | tf_op jit(solution)/shard_map/psum | solution.py:121
  70.3 17.3 %while.10 = (s32[]{:T(128)}, f32[4,32,3,128]{3,2,1,0:T(4,128)S(1)}, bf16[4,32,3,256]{3,2,1,0:T(4,128)(2,1)S(1)}, s32[4,32]{1,0:T(4,128)S(1)}, bf16[32,256,128]{2,1,0:T(8,128)(2,1)S(1)}, /*index=5*/s32[]{:T(128)}) while((s32[]{:T(128)}, f32[4,32,3,128]{3,2,1,0:T(4,128)S(1)}, bf16[4,32,3,256]{3,2,1,0:T(4,128)(2,1)S(1)}, s32[4,32]{1,0:T(4,128)S(1)}, ...), condition=%wide.region_8.9_spmd, body=%wide.region_7.8_spmd.sunk | while | flops 7341346 | bytes 6428917 | solution.py:86
  88.9 3.5 %psum.65 = f32[3,32,128]{2,1,0:T(8,128)S(1)} all-reduce(f32[3,32,128]{2,1,0:T(8,128)S(1)} %reshape.93), channel_id=1, replica_groups=mesh['grp'=2,'gx'=4,'gy'=2,'gz'=2] {'gz'}, use_global_device_ids=true, to_apply=%region_9.10 | all-reduce | flops 12288 | bytes 98304 | tf_op jit(solution)/shard_map/psum | solution.py:159
  95.4 4.2 %collective-permute-done.1 = f32[3,16,1,128]{3,1,2,0:T(8,128)S(1)} collective-permute-done((f32[3,16,1,128]{3,1,2,0:T(8,128)S(1)}, f32[3,16,1,128]{3,1,2,0:T(8,128)S(1)}, u32[]{:S(2)}, u32[]{:S(2)}) %collective-permute-start.1) | collective-permute-done | bytes 24608 | tf_op jit(solution)/shard_map/ppermute | solution.py:26
  104.0 3.9 %collective-permute-done.3 = f32[3,16,34,1]{2,1,3,0:T(8,128)S(1)} collective-permute-done((f32[3,16,34,1]{2,1,3,0:T(8,128)S(1)}, f32[3,16,34,1]{2,1,3,0:T(8,128)S(1)}, u32[]{:S(2)}, u32[]{:S(2)}) %collective-permute-start.3) | collective-permute-done | bytes 6560 | tf_op jit(solution)/shard_map/ppermute | solution.py:26
  119.3 4.2 %collective-permute-done.6 = f32[16,1,128]{2,0,1:T(8,128)S(1)} collective-permute-done((f32[16,1,128]{2,0,1:T(8,128)S(1)}, f32[16,1,128]{2,0,1:T(8,128)S(1)}, u32[]{:S(2)}, u32[]{:S(2)}) %collective-permute-start.6) | collective-permute-done | bytes 8224 | tf_op jit(solution)/shard_map/ppermute | solution.py:26
  127.1 3.3 collective-permute-done.9
  130.3 4.1 %collective-permute-done.8 = f32[16,34,1]{2,0,1:T(8,128)S(1)} collective-permute-done((f32[16,34,1]{2,0,1:T(8,128)S(1)}, f32[16,34,1]{2,0,1:T(8,128)S(1)}, u32[]{:S(2)}, u32[]{:S(2)}) %collective-permute-start.8) | collective-permute-done | bytes 2208 | tf_op jit(solution)/shard_map/ppermute | solution.py:26
  136.1 3.3 collective-permute-start.11
  141.7 30.5 %all-reduce.2 = (f32[]{:T(128)}, f32[]{:T(128)}) all-reduce(f32[]{:T(128)} %get-tuple-element.41, f32[]{:T(128)} %get-tuple-element.40), channel_id=1, replica_groups=mesh['grp'=2,'gx'=4,'gy'=2,'gz'=2] {'gx','gy','gz'}, use_global_device_ids=true, to_apply=%region_11.12 | all-reduce | flops 2 | bytes 16 | tf_op jit(solution)/shard_map/psum | solution.py:91
  176.5 4.2 %collective-permute-done.13 = f32[3,16,1,128]{3,1,2,0:T(8,128)S(1)} collective-permute-done((f32[3,16,1,128]{3,1,2,0:T(8,128)S(1)}, f32[3,16,1,128]{3,1,2,0:T(8,128)S(1)}, u32[]{:S(2)}, u32[]{:S(2)}) %collective-permute-start.13) | collective-permute-done | bytes 24608 | tf_op jit(solution)/shard_map/ppermute | solution.py:26
  186.3 4.0 %collective-permute-done.15 = f32[3,16,34,1]{2,1,3,0:T(8,128)} collective-permute-done((f32[3,16,34,1]{2,1,3,0:T(8,128)S(1)}, f32[3,16,34,1]{2,1,3,0:T(8,128)}, u32[]{:S(2)}, u32[]{:S(2)}) %collective-permute-start.15) | collective-permute-done | bytes 6560 | tf_op jit(solution)/shard_map/ppermute | solution.py:26
  202.7 4.2 %collective-permute-done.18 = f32[16,1,128]{2,0,1:T(8,128)S(1)} collective-permute-done((f32[16,1,128]{2,0,1:T(8,128)S(1)}, f32[16,1,128]{2,0,1:T(8,128)S(1)}, u32[]{:S(2)}, u32[]{:S(2)}) %collective-permute-start.18) | collective-permute-done | bytes 8224 | tf_op jit(solution)/shard_map/ppermute | solution.py:26
  213.5 4.1 %collective-permute-done.20 = f32[16,34,1]{2,0,1:T(8,128)S(1)} collective-permute-done((f32[16,34,1]{2,0,1:T(8,128)S(1)}, f32[16,34,1]{2,0,1:T(8,128)S(1)}, u32[]{:S(2)}, u32[]{:S(2)}) %collective-permute-start.20) | collective-permute-done | bytes 2208 | tf_op jit(solution)/shard_map/ppermute | solution.py:26
  225.0 30.5 %all-reduce.1 = (f32[]{:T(128)}, f32[]{:T(128)}) all-reduce(f32[]{:T(128)} %get-tuple-element.39, f32[]{:T(128)} %get-tuple-element.38), channel_id=1, replica_groups=mesh['grp'=2,'gx'=4,'gy'=2,'gz'=2] {'gx','gy','gz'}, use_global_device_ids=true, to_apply=%region_15.16 | all-reduce | flops 2 | bytes 16 | tf_op jit(solution)/shard_map/psum | solution.py:91
  263.0 4.2 %collective-permute-done.25 = f32[3,16,1,128]{3,1,2,0:T(8,128)S(1)} collective-permute-done((f32[3,16,1,128]{3,1,2,0:T(8,128)S(1)}, f32[3,16,1,128]{3,1,2,0:T(8,128)S(1)}, u32[]{:S(2)}, u32[]{:S(2)}) %collective-permute-start.25) | collective-permute-done | bytes 24608 | tf_op jit(solution)/shard_map/ppermute | solution.py:26
  273.8 3.8 %collective-permute-done.27 = f32[3,16,34,1]{2,1,3,0:T(8,128)} collective-permute-done((f32[3,16,34,1]{2,1,3,0:T(8,128)S(1)}, f32[3,16,34,1]{2,1,3,0:T(8,128)}, u32[]{:S(2)}, u32[]{:S(2)}) %collective-permute-start.27) | collective-permute-done | bytes 6560 | tf_op jit(solution)/shard_map/ppermute | solution.py:26
  290.0 4.2 %collective-permute-done.30 = f32[16,1,128]{2,0,1:T(8,128)S(1)} collective-permute-done((f32[16,1,128]{2,0,1:T(8,128)S(1)}, f32[16,1,128]{2,0,1:T(8,128)S(1)}, u32[]{:S(2)}, u32[]{:S(2)}) %collective-permute-start.30) | collective-permute-done | bytes 8224 | tf_op jit(solution)/shard_map/ppermute | solution.py:26
  300.8 4.1 %collective-permute-done.32 = f32[16,34,1]{2,0,1:T(8,128)S(1)} collective-permute-done((f32[16,34,1]{2,0,1:T(8,128)S(1)}, f32[16,34,1]{2,0,1:T(8,128)S(1)}, u32[]{:S(2)}, u32[]{:S(2)}) %collective-permute-start.32) | collective-permute-done | bytes 2208 | tf_op jit(solution)/shard_map/ppermute | solution.py:26
  312.4 30.4 %all-reduce = (f32[]{:T(128)}, f32[]{:T(128)}) all-reduce(f32[]{:T(128)} %get-tuple-element.37, f32[]{:T(128)} %get-tuple-element.36), channel_id=1, replica_groups=mesh['grp'=2,'gx'=4,'gy'=2,'gz'=2] {'gx','gy','gz'}, use_global_device_ids=true, to_apply=%region_19.20 | all-reduce | flops 2 | bytes 16 | tf_op jit(solution)/shard_map/psum | solution.py:91
  (202 shorter events, 131.8 us)
Async XLA Ops:
  3.7 13.7 %all-to-all-start.2 = ((s32[8,1,16]{2,1,0:T(1,128)}), s32[8,1,16]{2,1,0:T(1,128)S(1)}, u32[]{:S(2)}, u32[]{:S(2)}) async-start(s32[8,1,16]{2,1,0:T(1,128)} %bitcast.17), calls=%async_computation.2 | async-start | bytes 8192 | tf_op jit(solution)/shard_map/all_to_all | solution.py:142
  17.4 10.1 %all-to-all-start = ((s32[8,1,16]{2,1,0:T(1,128)}), s32[8,1,16]{2,1,0:T(1,128)S(1)}, u32[]{:S(2)}, u32[]{:S(2)}) async-start(s32[8,1,16]{2,1,0:T(1,128)} %bitcast.8), calls=%async_computation | async-start | bytes 8192 | tf_op jit(solution)/shard_map/all_to_all | solution.py:143
  27.4 41.5 %all-to-all-start.1 = ((f32[8,16,4,256]{3,1,2,0:T(8,128)}), f32[8,16,4,256]{3,1,2,0:T(8,128)S(1)}, u32[]{:S(2)}, u32[]{:S(2)}) async-start(f32[8,16,4,256]{3,1,2,0:T(8,128)} %copy.111), calls=%async_computation.1 | async-start | bytes 1048576 | tf_op jit(solution)/shard_map/all_to_all | solution.py:141
  93.9 5.7 %collective-permute-start.1 = (f32[3,16,1,128]{3,1,2,0:T(8,128)S(1)}, f32[3,16,1,128]{3,1,2,0:T(8,128)S(1)}, u32[]{:S(2)}, u32[]{:S(2)}) collective-permute-start(f32[3,16,1,128]{3,1,2,0:T(8,128)S(1)} %get-tuple-element.100), channel_id=1, source_target_pairs={{4,0},{8,4},{12,8},{5,1},{9,5},{13,9},{6,2},{10,6},{14,10},{7,3},{... | collective-permute-start | bytes 73736 | tf_op jit(solution)/shard_map/ppermute | solution.py:26
  102.2 5.7 %collective-permute-start.3 = (f32[3,16,34,1]{2,1,3,0:T(8,128)S(1)}, f32[3,16,34,1]{2,1,3,0:T(8,128)S(1)}, u32[]{:S(2)}, u32[]{:S(2)}) collective-permute-start(f32[3,16,34,1]{2,1,3,0:T(8,128)S(1)} %copy.136), channel_id=1, source_target_pairs={{2,0},{3,1},{6,4},{7,5},{10,8},{11,9},{14,12},{15,13},{18,16},{19,... | collective-permute-start | bytes 19592 | tf_op jit(solution)/shard_map/ppermute | solution.py:26
  117.9 5.5 %collective-permute-start.6 = (f32[16,1,128]{2,0,1:T(8,128)S(1)}, f32[16,1,128]{2,0,1:T(8,128)S(1)}, u32[]{:S(2)}, u32[]{:S(2)}) collective-permute-start(f32[16,1,128]{2,0,1:T(8,128)S(1)} %get-tuple-element.112), channel_id=1, source_target_pairs={{4,0},{8,4},{12,8},{5,1},{9,5},{13,9},{6,2},{10,6},{14,10},{7,3},{... | collective-permute-start | bytes 24584 | tf_op jit(solution)/shard_map/ppermute | solution.py:26
  123.6 6.7 %collective-permute-start.9 = (f32[16,34,1]{2,0,1:T(8,128)S(1)}, f32[16,34,1]{2,0,1:T(8,128)S(1)}, u32[]{:S(2)}, u32[]{:S(2)}) collective-permute-start(f32[16,34,1]{2,0,1:T(8,128)S(1)} %get-tuple-element.105), channel_id=1, source_target_pairs={{0,2},{1,3},{4,6},{5,7},{8,10},{9,11},{12,14},{13,15},{16,18},{17,... | collective-permute-start | bytes 6536 | tf_op jit(solution)/shard_map/ppermute | solution.py:24
  125.3 9.2 %collective-permute-start.8 = (f32[16,34,1]{2,0,1:T(8,128)S(1)}, f32[16,34,1]{2,0,1:T(8,128)S(1)}, u32[]{:S(2)}, u32[]{:S(2)}) collective-permute-start(f32[16,34,1]{2,0,1:T(8,128)S(1)} %get-tuple-element.106), channel_id=1, source_target_pairs={{2,0},{3,1},{6,4},{7,5},{10,8},{11,9},{14,12},{15,13},{18,16},{19,... | collective-permute-start | bytes 6536 | tf_op jit(solution)/shard_map/ppermute | solution.py:26
  134.8 5.3 %collective-permute-start.10 = (f32[1,34,130]{2,0,1:T(1,128)S(1)}, f32[1,34,130]{2,0,1:T(1,128)S(1)}, u32[]{:S(2)}, u32[]{:S(2)}) collective-permute-start(f32[1,34,130]{2,0,1:T(1,128)S(1)} %get-tuple-element.89), channel_id=1, source_target_pairs={{1,0},{3,2},{5,4},{7,6},{9,8},{11,10},{13,12},{15,14},{17,16},{19,... | collective-permute-start | bytes 53048 | tf_op jit(solution)/shard_map/ppermute | solution.py:26
  136.1 4.0 %collective-permute-start.11 = (f32[1,34,130]{2,0,1:T(1,128)S(1)}, f32[1,34,130]{2,0,1:T(1,128)S(1)}, u32[]{:S(2)}, u32[]{:S(2)}) collective-permute-start(f32[1,34,130]{2,0,1:T(1,128)S(1)} %get-tuple-element.90), channel_id=1, source_target_pairs={{0,1},{2,3},{4,5},{6,7},{8,9},{10,11},{12,13},{14,15},{16,17},{18,... | collective-permute-start | bytes 53048 | tf_op jit(solution)/shard_map/ppermute | solution.py:24
  175.0 5.7 %collective-permute-start.13 = (f32[3,16,1,128]{3,1,2,0:T(8,128)S(1)}, f32[3,16,1,128]{3,1,2,0:T(8,128)S(1)}, u32[]{:S(2)}, u32[]{:S(2)}) collective-permute-start(f32[3,16,1,128]{3,1,2,0:T(8,128)S(1)} %get-tuple-element.98), channel_id=1, source_target_pairs={{4,0},{8,4},{12,8},{5,1},{9,5},{13,9},{6,2},{10,6},{14,10},{7,3},{... | collective-permute-start | bytes 73736 | tf_op jit(solution)/shard_map/ppermute | solution.py:26
  184.5 5.8 %collective-permute-start.15 = (f32[3,16,34,1]{2,1,3,0:T(8,128)S(1)}, f32[3,16,34,1]{2,1,3,0:T(8,128)}, u32[]{:S(2)}, u32[]{:S(2)}) collective-permute-start(f32[3,16,34,1]{2,1,3,0:T(8,128)S(1)} %copy.138), channel_id=1, source_target_pairs={{2,0},{3,1},{6,4},{7,5},{10,8},{11,9},{14,12},{15,13},{18,16},{19,... | collective-permute-start | bytes 19592 | tf_op jit(solution)/shard_map/ppermute | solution.py:26
  201.4 5.5 %collective-permute-start.18 = (f32[16,1,128]{2,0,1:T(8,128)S(1)}, f32[16,1,128]{2,0,1:T(8,128)S(1)}, u32[]{:S(2)}, u32[]{:S(2)}) collective-permute-start(f32[16,1,128]{2,0,1:T(8,128)S(1)} %get-tuple-element.110), channel_id=1, source_target_pairs={{4,0},{8,4},{12,8},{5,1},{9,5},{13,9},{6,2},{10,6},{14,10},{7,3},{... | collective-permute-start | bytes 24584 | tf_op jit(solution)/shard_map/ppermute | solution.py:26
  207.1 6.5 %collective-permute-start.21 = (f32[16,34,1]{2,0,1:T(8,128)S(1)}, f32[16,34,1]{2,0,1:T(8,128)S(1)}, u32[]{:S(2)}, u32[]{:S(2)}) collective-permute-start(f32[16,34,1]{2,0,1:T(8,128)S(1)} %get-tuple-element.103), channel_id=1, source_target_pairs={{0,2},{1,3},{4,6},{5,7},{8,10},{9,11},{12,14},{13,15},{16,18},{17,... | collective-permute-start | bytes 6536 | tf_op jit(solution)/shard_map/ppermute | solution.py:24
  208.6 9.0 %collective-permute-start.20 = (f32[16,34,1]{2,0,1:T(8,128)S(1)}, f32[16,34,1]{2,0,1:T(8,128)S(1)}, u32[]{:S(2)}, u32[]{:S(2)}) collective-permute-start(f32[16,34,1]{2,0,1:T(8,128)S(1)} %get-tuple-element.104), channel_id=1, source_target_pairs={{2,0},{3,1},{6,4},{7,5},{10,8},{11,9},{14,12},{15,13},{18,16},{19,... | collective-permute-start | bytes 6536 | tf_op jit(solution)/shard_map/ppermute | solution.py:26
  218.0 5.1 %collective-permute-start.22 = (f32[1,34,130]{2,0,1:T(1,128)S(1)}, f32[1,34,130]{2,0,1:T(1,128)S(1)}, u32[]{:S(2)}, u32[]{:S(2)}) collective-permute-start(f32[1,34,130]{2,0,1:T(1,128)S(1)} %get-tuple-element.85), channel_id=1, source_target_pairs={{1,0},{3,2},{5,4},{7,6},{9,8},{11,10},{13,12},{15,14},{17,16},{19,... | collective-permute-start | bytes 53048 | tf_op jit(solution)/shard_map/ppermute | solution.py:26
  219.3 4.0 %collective-permute-start.23 = (f32[1,34,130]{2,0,1:T(1,128)S(1)}, f32[1,34,130]{2,0,1:T(1,128)S(1)}, u32[]{:S(2)}, u32[]{:S(2)}) collective-permute-start(f32[1,34,130]{2,0,1:T(1,128)S(1)} %get-tuple-element.86), channel_id=1, source_target_pairs={{0,1},{2,3},{4,5},{6,7},{8,9},{10,11},{12,13},{14,15},{16,17},{18,... | collective-permute-start | bytes 53048 | tf_op jit(solution)/shard_map/ppermute | solution.py:24
  261.5 5.7 %collective-permute-start.25 = (f32[3,16,1,128]{3,1,2,0:T(8,128)S(1)}, f32[3,16,1,128]{3,1,2,0:T(8,128)S(1)}, u32[]{:S(2)}, u32[]{:S(2)}) collective-permute-start(f32[3,16,1,128]{3,1,2,0:T(8,128)S(1)} %get-tuple-element.96), channel_id=1, source_target_pairs={{4,0},{8,4},{12,8},{5,1},{9,5},{13,9},{6,2},{10,6},{14,10},{7,3},{... | collective-permute-start | bytes 73736 | tf_op jit(solution)/shard_map/ppermute | solution.py:26
  271.8 5.8 %collective-permute-start.27 = (f32[3,16,34,1]{2,1,3,0:T(8,128)S(1)}, f32[3,16,34,1]{2,1,3,0:T(8,128)}, u32[]{:S(2)}, u32[]{:S(2)}) collective-permute-start(f32[3,16,34,1]{2,1,3,0:T(8,128)S(1)} %copy.140), channel_id=1, source_target_pairs={{2,0},{3,1},{6,4},{7,5},{10,8},{11,9},{14,12},{15,13},{18,16},{19,... | collective-permute-start | bytes 19592 | tf_op jit(solution)/shard_map/ppermute | solution.py:26
  288.7 5.5 %collective-permute-start.30 = (f32[16,1,128]{2,0,1:T(8,128)S(1)}, f32[16,1,128]{2,0,1:T(8,128)S(1)}, u32[]{:S(2)}, u32[]{:S(2)}) collective-permute-start(f32[16,1,128]{2,0,1:T(8,128)S(1)} %get-tuple-element.108), channel_id=1, source_target_pairs={{4,0},{8,4},{12,8},{5,1},{9,5},{13,9},{6,2},{10,6},{14,10},{7,3},{... | collective-permute-start | bytes 24584 | tf_op jit(solution)/shard_map/ppermute | solution.py:26
  294.4 6.4 %collective-permute-start.33 = (f32[16,34,1]{2,0,1:T(8,128)S(1)}, f32[16,34,1]{2,0,1:T(8,128)S(1)}, u32[]{:S(2)}, u32[]{:S(2)}) collective-permute-start(f32[16,34,1]{2,0,1:T(8,128)S(1)} %get-tuple-element.101), channel_id=1, source_target_pairs={{0,2},{1,3},{4,6},{5,7},{8,10},{9,11},{12,14},{13,15},{16,18},{17,... | collective-permute-start | bytes 6536 | tf_op jit(solution)/shard_map/ppermute | solution.py:24
  295.9 9.0 %collective-permute-start.32 = (f32[16,34,1]{2,0,1:T(8,128)S(1)}, f32[16,34,1]{2,0,1:T(8,128)S(1)}, u32[]{:S(2)}, u32[]{:S(2)}) collective-permute-start(f32[16,34,1]{2,0,1:T(8,128)S(1)} %get-tuple-element.102), channel_id=1, source_target_pairs={{2,0},{3,1},{6,4},{7,5},{10,8},{11,9},{14,12},{15,13},{18,16},{19,... | collective-permute-start | bytes 6536 | tf_op jit(solution)/shard_map/ppermute | solution.py:26
  305.2 5.2 %collective-permute-start.34 = (f32[1,34,130]{2,0,1:T(1,128)S(1)}, f32[1,34,130]{2,0,1:T(1,128)S(1)}, u32[]{:S(2)}, u32[]{:S(2)}) collective-permute-start(f32[1,34,130]{2,0,1:T(1,128)S(1)} %get-tuple-element.81), channel_id=1, source_target_pairs={{1,0},{3,2},{5,4},{7,6},{9,8},{11,10},{13,12},{15,14},{17,16},{19,... | collective-permute-start | bytes 53048 | tf_op jit(solution)/shard_map/ppermute | solution.py:26
  306.6 4.0 %collective-permute-start.35 = (f32[1,34,130]{2,0,1:T(1,128)S(1)}, f32[1,34,130]{2,0,1:T(1,128)S(1)}, u32[]{:S(2)}, u32[]{:S(2)}) collective-permute-start(f32[1,34,130]{2,0,1:T(1,128)S(1)} %get-tuple-element.82), channel_id=1, source_target_pairs={{0,1},{2,3},{4,5},{6,7},{8,9},{10,11},{12,13},{14,15},{16,17},{18,... | collective-permute-start | bytes 53048 | tf_op jit(solution)/shard_map/ppermute | solution.py:24
  (33 other events, 427.8 us)
where the time goes:
time: 351 us; the launch traced here: 349 us
  blocking collectives  130 us (37%)
  waiting for transfers between devices  73.2 us (21%)
  starting transfers between devices  70.3 us (20%)
  local copies, waits for them, and re-layouts  26.9 us (8%)
  other arithmetic  26.2 us (7%)
  between operations  12.4 us (4%)
  matrix products  10.8 us (3%)
    psum x3, blocking collectives, two_products(): lax.psum((jnp.sum(residual * residual), jnp.sum(residual * image)), ('gx'...  91.4 us
    ppermute x18, waiting for transfers between devices, extended(): lax.ppermute(head, axis, [((i + 1) % count, i) for i in range(ends)])  55 us
    psum x1, blocking collectives, per_device(): lax.psum((jnp.sum(resid * resid), jnp.sum(valid)), ('gx', 'gy', 'gz'))  34.7 us
    ppermute x18, starting transfers between devices, extended(): lax.ppermute(tail, axis, [(i, (i + 1) % count) for i in range(ends)])  32.4 us
    ppermute x18, starting transfers between devices, extended(): lax.ppermute(head, axis, [((i + 1) % count, i) for i in range(ends)])  23.5 us
    ppermute x18, waiting for transfers between devices, extended(): lax.ppermute(tail, axis, [(i, (i + 1) % count) for i in range(ends)])  10.7 us
    gather x4, local copies, waits for them, and re-layouts, per_group(): selected_entries = jnp.take(weights, block_tables, axis=0)  8.72 us
    dot_general x4, matrix products, per_group(): jnp.einsum('aow,awv->aov', block_coefficient_values, selected_entries, pr...  8.3 us
  transfers between devices with their start and end apart: 39, of which 25 were waited for; matrix products, arithmetic and copies ran while one was open for 4% of the time, Pallas kernels for 0%

commit v1 on v0

--- a/solution.py
+++ b/solution.py
@@ -118,7 +118,9 @@
     column = lax.broadcasted_iota(jnp.int32, (blocks, pixels), 1)
     valid = coherence_mask.astype(jnp.float32) * (column < block_count[:, None]).astype(jnp.float32)
     resid = (predicted - observed) * valid[:, None, :]
-    misfit, weight = lax.psum((jnp.sum(resid * resid), jnp.sum(valid)), ("gx", "gy", "gz"))
+    misfit, weight = lax.psum(
+        lax.psum((jnp.sum(resid * resid), jnp.sum(valid)), ("gy", "gz")), "gx"
+    )
     scale = lax.rsqrt(misfit / (EPOCHS * weight) + EPS)
     owner = block_owner[:, 0]
     order = lax.broadcasted_iota(jnp.int32, (blocks, blocks), 0)

time: 351 us -> 339 us (0.966)
  blocking collectives: 130 us -> 116 us
    psum x1 -> x2, blocking collectives: 34.7 us -> 20.6 us  [the longest x1 12.6 us: per_device(): lax.psum(lax.psum((jnp.sum(resid * resid), jnp.sum(valid)), ('gy', 'gz'))...]
where the time goes in v1:
time: 339 us; the launch traced here: 337 us
  blocking collectives  116 us (34%)
  waiting for transfers between devices  72.9 us (22%)
  starting transfers between devices  71.5 us (21%)
  local copies, waits for them, and re-layouts  26.9 us (8%)
  other arithmetic  26.3 us (8%)
  between operations  12.9 us (4%)
  matrix products  10.8 us (3%)
    psum x3, blocking collectives, two_products(): lax.psum((jnp.sum(residual * residual), jnp.sum(residual * image)), ('gx'...  91.4 us
    ppermute x18, waiting for transfers between devices, extended(): lax.ppermute(head, axis, [((i + 1) % count, i) for i in range(ends)])  55 us
    ppermute x18, starting transfers between devices, extended(): lax.ppermute(tail, axis, [(i, (i + 1) % count) for i in range(ends)])  33.7 us
    ppermute x18, starting transfers between devices, extended(): lax.ppermute(head, axis, [((i + 1) % count, i) for i in range(ends)])  23.5 us
    psum x1, blocking collectives, per_device(): lax.psum(lax.psum((jnp.sum(resid * resid), jnp.sum(valid)), ('gy', 'gz'))...  12.6 us
    ppermute x18, waiting for transfers between devices, extended(): lax.ppermute(tail, axis, [(i, (i + 1) % count) for i in range(ends)])  10.4 us
    gather x4, local copies, waits for them, and re-layouts, per_group(): selected_entries = jnp.take(weights, block_tables, axis=0)  8.68 us
    dot_general x4, matrix products, per_group(): jnp.einsum('aow,awv->aov', block_coefficient_values, selected_entries, pr...  8.3 us
  transfers between devices with their start and end apart: 39, of which 25 were waited for; matrix products, arithmetic and copies ran while one was open for 4% of the time, Pallas kernels for 0%

profile of v1, /device:TPU:0, one launch (start us, length us, event | category | flops | bytes accessed | tf_op | source)
XLA Modules:
  0.0 337.0 jit_solution(11320903060627053850)
XLA Ops:
  3.7 7.3 %all-to-all-start.2 = ((s32[8,1,16]{2,1,0:T(1,128)}), s32[8,1,16]{2,1,0:T(1,128)S(1)}, u32[]{:S(2)}, u32[]{:S(2)}) async-start(s32[8,1,16]{2,1,0:T(1,128)} %bitcast.17), calls=%async_computation.2 | async-start | bytes 8192 | tf_op jit(solution)/shard_map/all_to_all | solution.py:144
  17.4 3.6 %all-to-all-start = ((s32[8,1,16]{2,1,0:T(1,128)}), s32[8,1,16]{2,1,0:T(1,128)S(1)}, u32[]{:S(2)}, u32[]{:S(2)}) async-start(s32[8,1,16]{2,1,0:T(1,128)} %bitcast.8), calls=%async_computation | async-start | bytes 8192 | tf_op jit(solution)/shard_map/all_to_all | solution.py:145
  22.3 5.1 %all-to-all-done = s32[8,1,16]{2,1,0:T(1,128)S(1)} async-done(((s32[8,1,16]{2,1,0:T(1,128)}), s32[8,1,16]{2,1,0:T(1,128)S(1)}, u32[]{:S(2)}, u32[]{:S(2)}) %all-to-all-start) | async-done | bytes 544 | tf_op jit(solution)/shard_map/all_to_all | solution.py:145
  27.4 3.5 %all-to-all-start.1 = ((f32[8,16,4,256]{3,1,2,0:T(8,128)}), f32[8,16,4,256]{3,1,2,0:T(8,128)S(1)}, u32[]{:S(2)}, u32[]{:S(2)}) async-start(f32[8,16,4,256]{3,1,2,0:T(8,128)} %copy.111), calls=%async_computation.1 | async-start | bytes 1048576 | tf_op jit(solution)/shard_map/all_to_all | solution.py:143
  30.9 8.0 %all-reduce.3 = (f32[]{:T(128)}, f32[]{:T(128)}) all-reduce(f32[]{:T(128)} %get-tuple-element.66, f32[]{:T(128)} %get-tuple-element.64), channel_id=1, replica_groups=mesh['grp'=2,'gx'=4,'gy'=2,'gz'=2] {'gy','gz'}, use_global_device_ids=true, to_apply=%region_1.0 | all-reduce | flops 2 | bytes 16 | tf_op jit(solution)/shard_map/psum | solution.py:122
  38.9 12.6 %all-reduce.4 = (f32[]{:T(128)}, f32[]{:T(128)}) all-reduce(f32[]{:T(128)} %get-tuple-element.60, f32[]{:T(128)} %get-tuple-element.61), channel_id=1, replica_groups=mesh['grp'=2,'gx'=4,'gy'=2,'gz'=2] {'gx'}, use_global_device_ids=true, to_apply=%region_2.0 | all-reduce | flops 2 | bytes 16 | tf_op jit(solution)/shard_map/psum | solution.py:121
  56.3 17.2 %while.10 = (s32[]{:T(128)}, f32[4,32,3,128]{3,2,1,0:T(4,128)S(1)}, bf16[4,32,3,256]{3,2,1,0:T(4,128)(2,1)S(1)}, s32[4,32]{1,0:T(4,128)S(1)}, bf16[32,256,128]{2,1,0:T(8,128)(2,1)S(1)}, /*index=5*/s32[]{:T(128)}) while((s32[]{:T(128)}, f32[4,32,3,128]{3,2,1,0:T(4,128)S(1)}, bf16[4,32,3,256]{3,2,1,0:T(4,128)(2,1)S(1)}, ...), condition=%wide.region_10.11_spmd, body=%wide.region_9.10_spmd.sunk | while | flops 7341346 | bytes 6428917 | solution.py:86
  74.9 3.5 %psum.81 = f32[3,32,128]{2,1,0:T(8,128)S(1)} all-reduce(f32[3,32,128]{2,1,0:T(8,128)S(1)} %reshape.93), channel_id=1, replica_groups=mesh['grp'=2,'gx'=4,'gy'=2,'gz'=2] {'gz'}, use_global_device_ids=true, to_apply=%region_11.12 | all-reduce | flops 12288 | bytes 98304 | tf_op jit(solution)/shard_map/psum | solution.py:161
  81.4 4.2 %collective-permute-done.1 = f32[3,16,1,128]{3,1,2,0:T(8,128)S(1)} collective-permute-done((f32[3,16,1,128]{3,1,2,0:T(8,128)S(1)}, f32[3,16,1,128]{3,1,2,0:T(8,128)S(1)}, u32[]{:S(2)}, u32[]{:S(2)}) %collective-permute-start.1) | collective-permute-done | bytes 24608 | tf_op jit(solution)/shard_map/ppermute | solution.py:26
  91.1 3.9 %collective-permute-done.3 = f32[3,16,34,1]{2,1,3,0:T(8,128)S(1)} collective-permute-done((f32[3,16,34,1]{2,1,3,0:T(8,128)S(1)}, f32[3,16,34,1]{2,1,3,0:T(8,128)S(1)}, u32[]{:S(2)}, u32[]{:S(2)}) %collective-permute-start.3) | collective-permute-done | bytes 6560 | tf_op jit(solution)/shard_map/ppermute | solution.py:26
  106.6 4.2 %collective-permute-done.6 = f32[16,1,128]{2,0,1:T(8,128)S(1)} collective-permute-done((f32[16,1,128]{2,0,1:T(8,128)S(1)}, f32[16,1,128]{2,0,1:T(8,128)S(1)}, u32[]{:S(2)}, u32[]{:S(2)}) %collective-permute-start.6) | collective-permute-done | bytes 8224 | tf_op jit(solution)/shard_map/ppermute | solution.py:26
  117.4 4.1 %collective-permute-done.8 = f32[16,34,1]{2,0,1:T(8,128)S(1)} collective-permute-done((f32[16,34,1]{2,0,1:T(8,128)S(1)}, f32[16,34,1]{2,0,1:T(8,128)S(1)}, u32[]{:S(2)}, u32[]{:S(2)}) %collective-permute-start.8) | collective-permute-done | bytes 2208 | tf_op jit(solution)/shard_map/ppermute | solution.py:26
  123.1 3.3 collective-permute-start.11
  128.8 30.5 %all-reduce.2 = (f32[]{:T(128)}, f32[]{:T(128)}) all-reduce(f32[]{:T(128)} %get-tuple-element.41, f32[]{:T(128)} %get-tuple-element.40), channel_id=1, replica_groups=mesh['grp'=2,'gx'=4,'gy'=2,'gz'=2] {'gx','gy','gz'}, use_global_device_ids=true, to_apply=%region_13.14 | all-reduce | flops 2 | bytes 16 | tf_op jit(solution)/shard_map/psum | solution.py:91
  163.5 4.2 %collective-permute-done.13 = f32[3,16,1,128]{3,1,2,0:T(8,128)S(1)} collective-permute-done((f32[3,16,1,128]{3,1,2,0:T(8,128)S(1)}, f32[3,16,1,128]{3,1,2,0:T(8,128)S(1)}, u32[]{:S(2)}, u32[]{:S(2)}) %collective-permute-start.13) | collective-permute-done | bytes 24608 | tf_op jit(solution)/shard_map/ppermute | solution.py:26
  173.3 4.0 %collective-permute-done.15 = f32[3,16,34,1]{2,1,3,0:T(8,128)} collective-permute-done((f32[3,16,34,1]{2,1,3,0:T(8,128)S(1)}, f32[3,16,34,1]{2,1,3,0:T(8,128)}, u32[]{:S(2)}, u32[]{:S(2)}) %collective-permute-start.15) | collective-permute-done | bytes 6560 | tf_op jit(solution)/shard_map/ppermute | solution.py:26
  189.7 4.2 %collective-permute-done.18 = f32[16,1,128]{2,0,1:T(8,128)S(1)} collective-permute-done((f32[16,1,128]{2,0,1:T(8,128)S(1)}, f32[16,1,128]{2,0,1:T(8,128)S(1)}, u32[]{:S(2)}, u32[]{:S(2)}) %collective-permute-start.18) | collective-permute-done | bytes 8224 | tf_op jit(solution)/shard_map/ppermute | solution.py:26
  200.5 4.1 %collective-permute-done.20 = f32[16,34,1]{2,0,1:T(8,128)S(1)} collective-permute-done((f32[16,34,1]{2,0,1:T(8,128)S(1)}, f32[16,34,1]{2,0,1:T(8,128)S(1)}, u32[]{:S(2)}, u32[]{:S(2)}) %collective-permute-start.20) | collective-permute-done | bytes 2208 | tf_op jit(solution)/shard_map/ppermute | solution.py:26
  212.0 30.5 %all-reduce.1 = (f32[]{:T(128)}, f32[]{:T(128)}) all-reduce(f32[]{:T(128)} %get-tuple-element.39, f32[]{:T(128)} %get-tuple-element.38), channel_id=1, replica_groups=mesh['grp'=2,'gx'=4,'gy'=2,'gz'=2] {'gx','gy','gz'}, use_global_device_ids=true, to_apply=%region_17.18 | all-reduce | flops 2 | bytes 16 | tf_op jit(solution)/shard_map/psum | solution.py:91
  250.3 4.2 %collective-permute-done.25 = f32[3,16,1,128]{3,1,2,0:T(8,128)S(1)} collective-permute-done((f32[3,16,1,128]{3,1,2,0:T(8,128)S(1)}, f32[3,16,1,128]{3,1,2,0:T(8,128)S(1)}, u32[]{:S(2)}, u32[]{:S(2)}) %collective-permute-start.25) | collective-permute-done | bytes 24608 | tf_op jit(solution)/shard_map/ppermute | solution.py:26
  261.2 3.8 %collective-permute-done.27 = f32[3,16,34,1]{2,1,3,0:T(8,128)} collective-permute-done((f32[3,16,34,1]{2,1,3,0:T(8,128)S(1)}, f32[3,16,34,1]{2,1,3,0:T(8,128)}, u32[]{:S(2)}, u32[]{:S(2)}) %collective-permute-start.27) | collective-permute-done | bytes 6560 | tf_op jit(solution)/shard_map/ppermute | solution.py:26
  277.3 4.2 %collective-permute-done.30 = f32[16,1,128]{2,0,1:T(8,128)S(1)} collective-permute-done((f32[16,1,128]{2,0,1:T(8,128)S(1)}, f32[16,1,128]{2,0,1:T(8,128)S(1)}, u32[]{:S(2)}, u32[]{:S(2)}) %collective-permute-start.30) | collective-permute-done | bytes 8224 | tf_op jit(solution)/shard_map/ppermute | solution.py:26
  288.1 4.1 %collective-permute-done.32 = f32[16,34,1]{2,0,1:T(8,128)S(1)} collective-permute-done((f32[16,34,1]{2,0,1:T(8,128)S(1)}, f32[16,34,1]{2,0,1:T(8,128)S(1)}, u32[]{:S(2)}, u32[]{:S(2)}) %collective-permute-start.32) | collective-permute-done | bytes 2208 | tf_op jit(solution)/shard_map/ppermute | solution.py:26
  299.7 30.4 %all-reduce = (f32[]{:T(128)}, f32[]{:T(128)}) all-reduce(f32[]{:T(128)} %get-tuple-element.37, f32[]{:T(128)} %get-tuple-element.36), channel_id=1, replica_groups=mesh['grp'=2,'gx'=4,'gy'=2,'gz'=2] {'gx','gy','gz'}, use_global_device_ids=true, to_apply=%region_21.22 | all-reduce | flops 2 | bytes 16 | tf_op jit(solution)/shard_map/psum | solution.py:91
  (203 shorter events, 136.2 us)
Async XLA Ops:
  3.7 13.7 %all-to-all-start.2 = ((s32[8,1,16]{2,1,0:T(1,128)}), s32[8,1,16]{2,1,0:T(1,128)S(1)}, u32[]{:S(2)}, u32[]{:S(2)}) async-start(s32[8,1,16]{2,1,0:T(1,128)} %bitcast.17), calls=%async_computation.2 | async-start | bytes 8192 | tf_op jit(solution)/shard_map/all_to_all | solution.py:144
  17.4 10.0 %all-to-all-start = ((s32[8,1,16]{2,1,0:T(1,128)}), s32[8,1,16]{2,1,0:T(1,128)S(1)}, u32[]{:S(2)}, u32[]{:S(2)}) async-start(s32[8,1,16]{2,1,0:T(1,128)} %bitcast.8), calls=%async_computation | async-start | bytes 8192 | tf_op jit(solution)/shard_map/all_to_all | solution.py:145
  27.4 27.5 %all-to-all-start.1 = ((f32[8,16,4,256]{3,1,2,0:T(8,128)}), f32[8,16,4,256]{3,1,2,0:T(8,128)S(1)}, u32[]{:S(2)}, u32[]{:S(2)}) async-start(f32[8,16,4,256]{3,1,2,0:T(8,128)} %copy.111), calls=%async_computation.1 | async-start | bytes 1048576 | tf_op jit(solution)/shard_map/all_to_all | solution.py:143
  79.9 5.7 %collective-permute-start.1 = (f32[3,16,1,128]{3,1,2,0:T(8,128)S(1)}, f32[3,16,1,128]{3,1,2,0:T(8,128)S(1)}, u32[]{:S(2)}, u32[]{:S(2)}) collective-permute-start(f32[3,16,1,128]{3,1,2,0:T(8,128)S(1)} %get-tuple-element.102), channel_id=1, source_target_pairs={{4,0},{8,4},{12,8},{5,1},{9,5},{13,9},{6,2},{10,6},{14,10},{7,3},{... | collective-permute-start | bytes 73736 | tf_op jit(solution)/shard_map/ppermute | solution.py:26
  86.4 4.2 %collective-permute-start.2 = (f32[3,16,34,1]{2,1,3,0:T(8,128)S(1)}, f32[3,16,34,1]{2,1,3,0:T(8,128)S(1)}, u32[]{:S(2)}, u32[]{:S(2)}) collective-permute-start(f32[3,16,34,1]{2,1,3,0:T(8,128)S(1)} %copy.135), channel_id=1, source_target_pairs={{0,2},{1,3},{4,6},{5,7},{8,10},{9,11},{12,14},{13,15},{16,18},{17,... | collective-permute-start | bytes 19592 | tf_op jit(solution)/shard_map/ppermute | solution.py:24
  89.3 5.7 %collective-permute-start.3 = (f32[3,16,34,1]{2,1,3,0:T(8,128)S(1)}, f32[3,16,34,1]{2,1,3,0:T(8,128)S(1)}, u32[]{:S(2)}, u32[]{:S(2)}) collective-permute-start(f32[3,16,34,1]{2,1,3,0:T(8,128)S(1)} %copy.136), channel_id=1, source_target_pairs={{2,0},{3,1},{6,4},{7,5},{10,8},{11,9},{14,12},{15,13},{18,16},{19,... | collective-permute-start | bytes 19592 | tf_op jit(solution)/shard_map/ppermute | solution.py:26
  102.5 4.1 %collective-permute-start.7 = (f32[16,1,128]{2,0,1:T(8,128)S(1)}, f32[16,1,128]{2,0,1:T(8,128)S(1)}, u32[]{:S(2)}, u32[]{:S(2)}) collective-permute-start(f32[16,1,128]{2,0,1:T(8,128)S(1)} %get-tuple-element.113), channel_id=1, source_target_pairs={{0,4},{4,8},{8,12},{1,5},{5,9},{9,13},{2,6},{6,10},{10,14},{3,7},{... | collective-permute-start | bytes 24584 | tf_op jit(solution)/shard_map/ppermute | solution.py:24
  105.2 5.5 %collective-permute-start.6 = (f32[16,1,128]{2,0,1:T(8,128)S(1)}, f32[16,1,128]{2,0,1:T(8,128)S(1)}, u32[]{:S(2)}, u32[]{:S(2)}) collective-permute-start(f32[16,1,128]{2,0,1:T(8,128)S(1)} %get-tuple-element.114), channel_id=1, source_target_pairs={{4,0},{8,4},{12,8},{5,1},{9,5},{13,9},{6,2},{10,6},{14,10},{7,3},{... | collective-permute-start | bytes 24584 | tf_op jit(solution)/shard_map/ppermute | solution.py:26
  110.9 6.4 %collective-permute-start.9 = (f32[16,34,1]{2,0,1:T(8,128)S(1)}, f32[16,34,1]{2,0,1:T(8,128)S(1)}, u32[]{:S(2)}, u32[]{:S(2)}) collective-permute-start(f32[16,34,1]{2,0,1:T(8,128)S(1)} %get-tuple-element.107), channel_id=1, source_target_pairs={{0,2},{1,3},{4,6},{5,7},{8,10},{9,11},{12,14},{13,15},{16,18},{17,... | collective-permute-start | bytes 6536 | tf_op jit(solution)/shard_map/ppermute | solution.py:24
  112.6 8.9 %collective-permute-start.8 = (f32[16,34,1]{2,0,1:T(8,128)S(1)}, f32[16,34,1]{2,0,1:T(8,128)S(1)}, u32[]{:S(2)}, u32[]{:S(2)}) collective-permute-start(f32[16,34,1]{2,0,1:T(8,128)S(1)} %get-tuple-element.108), channel_id=1, source_target_pairs={{2,0},{3,1},{6,4},{7,5},{10,8},{11,9},{14,12},{15,13},{18,16},{19,... | collective-permute-start | bytes 6536 | tf_op jit(solution)/shard_map/ppermute | solution.py:26
  121.8 5.3 %collective-permute-start.10 = (f32[1,34,130]{2,0,1:T(1,128)S(1)}, f32[1,34,130]{2,0,1:T(1,128)S(1)}, u32[]{:S(2)}, u32[]{:S(2)}) collective-permute-start(f32[1,34,130]{2,0,1:T(1,128)S(1)} %get-tuple-element.91), channel_id=1, source_target_pairs={{1,0},{3,2},{5,4},{7,6},{9,8},{11,10},{13,12},{15,14},{17,16},{19,... | collective-permute-start | bytes 53048 | tf_op jit(solution)/shard_map/ppermute | solution.py:26
  123.1 4.0 %collective-permute-start.11 = (f32[1,34,130]{2,0,1:T(1,128)S(1)}, f32[1,34,130]{2,0,1:T(1,128)S(1)}, u32[]{:S(2)}, u32[]{:S(2)}) collective-permute-start(f32[1,34,130]{2,0,1:T(1,128)S(1)} %get-tuple-element.92), channel_id=1, source_target_pairs={{0,1},{2,3},{4,5},{6,7},{8,9},{10,11},{12,13},{14,15},{16,17},{18,... | collective-permute-start | bytes 53048 | tf_op jit(solution)/shard_map/ppermute | solution.py:24
  162.0 5.7 %collective-permute-start.13 = (f32[3,16,1,128]{3,1,2,0:T(8,128)S(1)}, f32[3,16,1,128]{3,1,2,0:T(8,128)S(1)}, u32[]{:S(2)}, u32[]{:S(2)}) collective-permute-start(f32[3,16,1,128]{3,1,2,0:T(8,128)S(1)} %get-tuple-element.100), channel_id=1, source_target_pairs={{4,0},{8,4},{12,8},{5,1},{9,5},{13,9},{6,2},{10,6},{14,10},{7,3},{... | collective-permute-start | bytes 73736 | tf_op jit(solution)/shard_map/ppermute | solution.py:26
  171.5 5.8 %collective-permute-start.15 = (f32[3,16,34,1]{2,1,3,0:T(8,128)S(1)}, f32[3,16,34,1]{2,1,3,0:T(8,128)}, u32[]{:S(2)}, u32[]{:S(2)}) collective-permute-start(f32[3,16,34,1]{2,1,3,0:T(8,128)S(1)} %copy.138), channel_id=1, source_target_pairs={{2,0},{3,1},{6,4},{7,5},{10,8},{11,9},{14,12},{15,13},{18,16},{19,... | collective-permute-start | bytes 19592 | tf_op jit(solution)/shard_map/ppermute | solution.py:26
  188.3 5.5 %collective-permute-start.18 = (f32[16,1,128]{2,0,1:T(8,128)S(1)}, f32[16,1,128]{2,0,1:T(8,128)S(1)}, u32[]{:S(2)}, u32[]{:S(2)}) collective-permute-start(f32[16,1,128]{2,0,1:T(8,128)S(1)} %get-tuple-element.112), channel_id=1, source_target_pairs={{4,0},{8,4},{12,8},{5,1},{9,5},{13,9},{6,2},{10,6},{14,10},{7,3},{... | collective-permute-start | bytes 24584 | tf_op jit(solution)/shard_map/ppermute | solution.py:26
  194.1 6.5 %collective-permute-start.21 = (f32[16,34,1]{2,0,1:T(8,128)S(1)}, f32[16,34,1]{2,0,1:T(8,128)S(1)}, u32[]{:S(2)}, u32[]{:S(2)}) collective-permute-start(f32[16,34,1]{2,0,1:T(8,128)S(1)} %get-tuple-element.105), channel_id=1, source_target_pairs={{0,2},{1,3},{4,6},{5,7},{8,10},{9,11},{12,14},{13,15},{16,18},{17,... | collective-permute-start | bytes 6536 | tf_op jit(solution)/shard_map/ppermute | solution.py:24
  195.6 9.0 %collective-permute-start.20 = (f32[16,34,1]{2,0,1:T(8,128)S(1)}, f32[16,34,1]{2,0,1:T(8,128)S(1)}, u32[]{:S(2)}, u32[]{:S(2)}) collective-permute-start(f32[16,34,1]{2,0,1:T(8,128)S(1)} %get-tuple-element.106), channel_id=1, source_target_pairs={{2,0},{3,1},{6,4},{7,5},{10,8},{11,9},{14,12},{15,13},{18,16},{19,... | collective-permute-start | bytes 6536 | tf_op jit(solution)/shard_map/ppermute | solution.py:26
  204.9 5.1 %collective-permute-start.22 = (f32[1,34,130]{2,0,1:T(1,128)S(1)}, f32[1,34,130]{2,0,1:T(1,128)S(1)}, u32[]{:S(2)}, u32[]{:S(2)}) collective-permute-start(f32[1,34,130]{2,0,1:T(1,128)S(1)} %get-tuple-element.87), channel_id=1, source_target_pairs={{1,0},{3,2},{5,4},{7,6},{9,8},{11,10},{13,12},{15,14},{17,16},{19,... | collective-permute-start | bytes 53048 | tf_op jit(solution)/shard_map/ppermute | solution.py:26
  248.8 5.7 %collective-permute-start.25 = (f32[3,16,1,128]{3,1,2,0:T(8,128)S(1)}, f32[3,16,1,128]{3,1,2,0:T(8,128)S(1)}, u32[]{:S(2)}, u32[]{:S(2)}) collective-permute-start(f32[3,16,1,128]{3,1,2,0:T(8,128)S(1)} %get-tuple-element.98), channel_id=1, source_target_pairs={{4,0},{8,4},{12,8},{5,1},{9,5},{13,9},{6,2},{10,6},{14,10},{7,3},{... | collective-permute-start | bytes 73736 | tf_op jit(solution)/shard_map/ppermute | solution.py:26
  259.1 5.8 %collective-permute-start.27 = (f32[3,16,34,1]{2,1,3,0:T(8,128)S(1)}, f32[3,16,34,1]{2,1,3,0:T(8,128)}, u32[]{:S(2)}, u32[]{:S(2)}) collective-permute-start(f32[3,16,34,1]{2,1,3,0:T(8,128)S(1)} %copy.140), channel_id=1, source_target_pairs={{2,0},{3,1},{6,4},{7,5},{10,8},{11,9},{14,12},{15,13},{18,16},{19,... | collective-permute-start | bytes 19592 | tf_op jit(solution)/shard_map/ppermute | solution.py:26
  276.0 5.5 %collective-permute-start.30 = (f32[16,1,128]{2,0,1:T(8,128)S(1)}, f32[16,1,128]{2,0,1:T(8,128)S(1)}, u32[]{:S(2)}, u32[]{:S(2)}) collective-permute-start(f32[16,1,128]{2,0,1:T(8,128)S(1)} %get-tuple-element.110), channel_id=1, source_target_pairs={{4,0},{8,4},{12,8},{5,1},{9,5},{13,9},{6,2},{10,6},{14,10},{7,3},{... | collective-permute-start | bytes 24584 | tf_op jit(solution)/shard_map/ppermute | solution.py:26
  281.7 6.4 %collective-permute-start.33 = (f32[16,34,1]{2,0,1:T(8,128)S(1)}, f32[16,34,1]{2,0,1:T(8,128)S(1)}, u32[]{:S(2)}, u32[]{:S(2)}) collective-permute-start(f32[16,34,1]{2,0,1:T(8,128)S(1)} %get-tuple-element.103), channel_id=1, source_target_pairs={{0,2},{1,3},{4,6},{5,7},{8,10},{9,11},{12,14},{13,15},{16,18},{17,... | collective-permute-start | bytes 6536 | tf_op jit(solution)/shard_map/ppermute | solution.py:24
  283.2 9.0 %collective-permute-start.32 = (f32[16,34,1]{2,0,1:T(8,128)S(1)}, f32[16,34,1]{2,0,1:T(8,128)S(1)}, u32[]{:S(2)}, u32[]{:S(2)}) collective-permute-start(f32[16,34,1]{2,0,1:T(8,128)S(1)} %get-tuple-element.104), channel_id=1, source_target_pairs={{2,0},{3,1},{6,4},{7,5},{10,8},{11,9},{14,12},{15,13},{18,16},{19,... | collective-permute-start | bytes 6536 | tf_op jit(solution)/shard_map/ppermute | solution.py:26
  292.6 5.2 %collective-permute-start.34 = (f32[1,34,130]{2,0,1:T(1,128)S(1)}, f32[1,34,130]{2,0,1:T(1,128)S(1)}, u32[]{:S(2)}, u32[]{:S(2)}) collective-permute-start(f32[1,34,130]{2,0,1:T(1,128)S(1)} %get-tuple-element.83), channel_id=1, source_target_pairs={{1,0},{3,2},{5,4},{7,6},{9,8},{11,10},{13,12},{15,14},{17,16},{19,... | collective-permute-start | bytes 53048 | tf_op jit(solution)/shard_map/ppermute | solution.py:26
  (33 other events, 388.2 us)
